TPU v7x, 32 devices: a 4x4x1 block of a 4x4x8 slice. The times are simulated.
32 devices in a mesh: batch: 1 (over z), stage: 4 (over y), seq: 8 (over x, core).
Axes of the slice: x: 4, y: 4, z: 1, core: 2. Of those that a mesh axis runs over, the one named last changes fastest.
The devices are a block of a 4x4x8 slice.
Arguments:
- x_tokens: bfloat16 [2, 8192, 1024], P('batch', 'seq')
- norm_attn: bfloat16 [4, 1024], P('stage')
- w_query: bfloat16 [4, 1024, 4096], P('stage')
- w_key: bfloat16 [4, 1024, 4096], P('stage')
- w_value: bfloat16 [4, 1024, 2048], P('stage')
- w_gate: bfloat16 [4, 1024, 32], P('stage')
- gate_bias: float32 [4, 32], P('stage')
- norm_out: bfloat16 [4, 64], P('stage')
- w_out: bfloat16 [4, 2048, 1024], P('stage')
- norm_mlp: bfloat16 [4, 1024], P('stage')
- w_up: bfloat16 [4, 1024, 4096], P('stage')
- w_down: bfloat16 [4, 4096, 1024], P('stage')
Outputs:
- output 1: bfloat16 [4, 2, 8192, 1024], P('stage', 'batch', 'seq')
- output 2: float32 [4, 2, 32, 128, 64], P('stage', 'batch')
All inputs are finite; a program needn't handle non-finite values.
Results may differ from a plain program's by a relative error of at most 0.02.
Values are sent between devices in bfloat16 or wider.
A program may use at most 768 MiB of HBM per device.

v0:
```python
import jax
import jax.numpy as jnp
from jax import lax
from jax.sharding import PartitionSpec as P

NORM_EPS = 1e-6


def rms_norm(values, gain_vec):
    mean_sq = jnp.mean(values * values, axis=-1, keepdims=True)
    return values * lax.rsqrt(mean_sq + NORM_EPS) * gain_vec.astype(jnp.float32)


def local_part(h_in, params):
    norm_attn, w_query, w_key, w_value, w_gate, gate_bias, norm_out, w_out, norm_mlp, w_up, w_down = params
    num_seqs, tok_len = h_in.shape[0], h_in.shape[1]
    num_heads = gate_bias.shape[0]
    key_dim = w_query.shape[1] // num_heads
    val_dim = norm_out.shape[0]
    h_f32 = h_in.astype(jnp.float32)
    u_norm = rms_norm(h_f32, norm_attn).astype(jnp.bfloat16)
    q_all = jnp.einsum('bcd,de->bce', u_norm, w_query, preferred_element_type=jnp.float32).astype(jnp.bfloat16)
    q_all = q_all.reshape(num_seqs, tok_len, num_heads, key_dim)
    k_raw = jnp.einsum('bcd,de->bce', u_norm, w_key, preferred_element_type=jnp.float32)
    k_all = (k_raw * key_dim ** -0.5).astype(jnp.bfloat16).reshape(num_seqs, tok_len, num_heads, key_dim)
    v_all = jnp.einsum('bcd,de->bce', u_norm, w_value, preferred_element_type=jnp.float32).astype(jnp.bfloat16)
    v_all = v_all.reshape(num_seqs, tok_len, num_heads, val_dim)
    gate_pre = jnp.einsum('bcd,dh->bch', u_norm, w_gate, preferred_element_type=jnp.float32) + gate_bias
    cum_decay = jnp.cumsum(jax.nn.log_sigmoid(gate_pre), axis=1)
    total_decay = cum_decay[:, -1, :]
    scores = jnp.einsum('bchk,bjhk->bhcj', q_all, k_all, preferred_element_type=jnp.float32)
    cum_heads = jnp.swapaxes(cum_decay, 1, 2)
    causal = jnp.arange(tok_len)[:, None] >= jnp.arange(tok_len)[None, :]
    decay_mat = jnp.exp(jnp.where(causal, cum_heads[:, :, :, None] - cum_heads[:, :, None, :], -jnp.inf))
    intra_out = jnp.einsum('bhcj,bjhv->bchv', scores * decay_mat, v_all, preferred_element_type=jnp.float32)
    k_decayed = k_all * jnp.exp(total_decay[:, None, :] - cum_decay)[..., None]
    local_state = jnp.einsum('bjhk,bjhv->bhkv', k_decayed, v_all, preferred_element_type=jnp.float32)
    return h_f32, q_all, cum_decay, total_decay, intra_out, local_state


def finish_part(h_f32, q_all, cum_decay, intra_out, state_in, params):
    norm_attn, w_query, w_key, w_value, w_gate, gate_bias, norm_out, w_out, norm_mlp, w_up, w_down = params
    num_seqs, tok_len = h_f32.shape[0], h_f32.shape[1]
    inter_out = jnp.einsum('bchk,bhkv->bchv', q_all, state_in, preferred_element_type=jnp.float32) * jnp.exp(cum_decay)[..., None]
    head_norm = rms_norm(inter_out + intra_out, norm_out).astype(jnp.bfloat16).reshape(num_seqs, tok_len, -1)
    h_mid = h_f32 + jnp.einsum('bce,ed->bcd', head_norm, w_out, preferred_element_type=jnp.float32)
    mlp_in = rms_norm(h_mid, norm_mlp).astype(jnp.bfloat16)
    hidden = jax.nn.gelu(jnp.einsum('bcd,df->bcf', mlp_in, w_up, preferred_element_type=jnp.float32), approximate=True).astype(jnp.bfloat16)
    return (h_mid + jnp.einsum('bcf,fd->bcd', hidden, w_down, preferred_element_type=jnp.float32)).astype(jnp.bfloat16)


def solution(mesh):
    num_stages = mesh.shape['stage']
    num_shards = mesh.shape['seq']
    step_count = num_stages + num_shards - 1
    stage_pairs = [(src_index, src_index + 1) for src_index in range(num_stages - 1)]
    seq_pairs = [(src_index, src_index + 1) for src_index in range(num_shards - 1)]
    mat_spec = P('stage', None, None)
    vec_spec = P('stage', None)
    weight_specs = (vec_spec, mat_spec, mat_spec, mat_spec, mat_spec, vec_spec, vec_spec, mat_spec, vec_spec, mat_spec, mat_spec)

    def device_program(x_tokens, norm_attn, w_query, w_key, w_value, w_gate, gate_bias, norm_out, w_out, norm_mlp, w_up, w_down):
        stage_idx = lax.axis_index('stage')
        seq_idx = lax.axis_index('seq')
        stacked = (norm_attn, w_query, w_key, w_value, w_gate, gate_bias, norm_out, w_out, norm_mlp, w_up, w_down)
        params = tuple(weight[0] for weight in stacked)
        num_seqs = x_tokens.shape[0]
        num_heads = gate_bias.shape[1]
        key_dim = w_query.shape[2] // num_heads
        val_dim = norm_out.shape[1]
        my_step = stage_idx + seq_idx

        def run_layer(operands):
            h_in, state_in = operands[0], operands[1]
            h_f32, q_all, cum_decay, total_decay, intra_out, local_state = local_part(h_in, params)
            state_out = jnp.exp(total_decay)[:, :, None, None] * state_in + local_state
            return finish_part(h_f32, q_all, cum_decay, intra_out, state_in, params), state_out

        def keep_layer(operands):
            return operands[2], operands[3]

        def step_body(step_num, loop_carry):
            h_recv, s_recv, y_done, s_done = loop_carry
            h_in = jnp.where(stage_idx == 0, x_tokens, h_recv)
            y_done, s_done = lax.cond(step_num == my_step, run_layer, keep_layer, (h_in, s_recv, y_done, s_done))
            h_recv = lax.ppermute(y_done, 'stage', stage_pairs)
            s_recv = lax.ppermute(s_done, 'seq', seq_pairs)
            return h_recv, s_recv, y_done, s_done

        zero_h = jnp.zeros_like(x_tokens)
        zero_s = jnp.zeros((num_seqs, num_heads, key_dim, val_dim), jnp.float32)
        loop_out = lax.fori_loop(0, step_count, step_body, (zero_h, zero_s, zero_h, zero_s))
        y_done, s_done = loop_out[2], loop_out[3]
        s_final = lax.psum(jnp.where(seq_idx == num_shards - 1, s_done, 0.0), 'seq')
        return y_done[None], s_final[None]

    return jax.shard_map(
        device_program,
        mesh=mesh,
        in_specs=(P('batch', 'seq', None),) + weight_specs,
        out_specs=(P('stage', 'batch', 'seq', None), P('stage', 'batch', None, None, None)),
        check_vma=False,
    )
```

profile of v0, /device:TPU:96, one launch (start us, length us, event | category | flops | bytes accessed | tf_op | source)
XLA Modules:
  0.0 3906.1 jit_solution(16030737653901199459)
XLA Ops:
  9.8 6.2 copy.81
  16.0 6.5 copy.80
  29.3 2840.1 %while.21 = (s32[]{:T(128)}, bf16[2,1024,1024]{1,2,0:T(8,128)(2,1)}, f32[2,32,128,64]{2,3,1,0:T(8,128)S(1)}, bf16[2,1024,1024]{1,2,0:T(8,128)(2,1)}, f32[2,32,12...) while((s32[]{:T(128)}, ...), condition=%wide.region_8.9_spmd, body=%wide.region_0.8_spmd.sunk | while | flops 114383601664 | bytes 463439936 | solution.py:92
  29.3 316.0 %conditional.2 = ((bf16[2,1024,1024]{1,2,0:T(8,128)(2,1)}, f32[2,32,128,64]{2,3,1,0:T(8,128)})) conditional(s32[]{:T(128)} %convert_element_type.109, (bf16[2,1024,1024]{1,2,0:T(8,128)(2,1)}, f32[2,32,128,64]{2,3,1,0:T(8,128)}) %tuple.57, (pred[]{:T(512)}, bf16[2,1024,1024]{1,2,0:T(8,128)(2,1)}, bf16[2,1024,1024]{1,2,0:T(8,128)(2,1)}, ...), branch_computations={%region_1.1_spmd, %region_2.7_spmd} | conditional | flops 114383601664 | bytes 438273728 | solution.py:85
  32.5 4.4 fusion.47
  41.1 18.0 reduce-window.4
  61.1 14.3 convolution_convert_fusion
  75.4 11.8 copy.72
  87.3 25.8 fusion.22
  113.0 13.4 multiply_add_fusion
  126.4 26.2 convert_bitcast_fusion
  152.6 12.7 fusion.28
  165.4 99.2 %multiply_reduce_fusion = (f32[2,1024,32]{1,2,0:T(8,128)S(1)}, f32[2,1024,32,64]{1,3,2,0:T(8,128)}) fusion(bf16[2,1024,32,64]{1,3,2,0:T(8,128)(2,1)} %bitcast.105, f32[2,32,1024]{2,1,0:T(8,128)S(1)} %reduce_window_sum.22, pred[1024,1024]{1,0:T(8,128)(4,1)S(1)} %iota_compare_fusion, bf16[2,128,32,8,128]{4,3,2,1,0:T(8,128)(2,1)} %fusion.22, ...), kind=kOutput, calls=%fused_computation.33 | convolution fusion | flops 25987842048 | bytes 77332480 | tf_op jit(solution)/shard_map/while/body/eval_jaxpr/cond/branch_1_fun/bhcj,bjhv->bchv/dot_general | solution.py:35
  264.7 9.0 multiply_convert_fusion.1
  273.8 11.3 multiply_reduce_fusion.1
  285.0 34.9 fusion.102
  319.9 24.9 add_convert_fusion
  350.0 3.6 collective-permute-done.1
  353.6 38.9 collective-permute-done
  392.8 8.3 conditional.2
  401.1 313.9 %collective-permute-start = (bf16[2,1024,1024]{1,2,0:T(8,128)(2,1)}, bf16[2,1024,1024]{1,2,0:T(8,128)(2,1)}, u32[]{:S(2)}, u32[]{:S(2)}) collective-permute-start(bf16[2,1024,1024]{1,2,0:T(8,128)(2,1)} %get-tuple-element.776), channel_id=1, source_target_pairs={{0,8},{8,16},{16,24},{1,9},{9,17},{17,25},{2,10},{10,18},{18,26},{... | collective-permute-start | bytes 12582920 | tf_op jit(solution)/shard_map/while/body/eval_jaxpr/ppermute | solution.py:86
  716.4 3.6 collective-permute-done.1
  720.1 41.5 %collective-permute-done = bf16[2,1024,1024]{1,2,0:T(8,128)(2,1)} collective-permute-done((bf16[2,1024,1024]{1,2,0:T(8,128)(2,1)}, bf16[2,1024,1024]{1,2,0:T(8,128)(2,1)}, u32[]{:S(2)}, u32[]{:S(2)}) %collective-permute-start) | collective-permute-done | bytes 4194336 | tf_op jit(solution)/shard_map/while/body/eval_jaxpr/ppermute | solution.py:86
  761.6 14.9 collective-permute-start
  776.5 267.1 %collective-permute-start.1 = (f32[2,32,128,64]{2,3,1,0:T(8,128)}, f32[2,32,128,64]{2,3,1,0:T(8,128)S(1)}, u32[]{:S(2)}, u32[]{:S(2)}) collective-permute-start(f32[2,32,128,64]{2,3,1,0:T(8,128)} %get-tuple-element.777), channel_id=1, source_target_pairs={{0,1},{1,2},{2,3},{3,4},{4,5},{5,6},{6,7},{8,9},{9,10},{10,11},{11... | collective-permute-start | bytes 6291464 | tf_op jit(solution)/shard_map/while/body/eval_jaxpr/ppermute | solution.py:87
  1043.6 3.6 collective-permute-done.1
  1047.2 86.8 %collective-permute-start = (bf16[2,1024,1024]{1,2,0:T(8,128)(2,1)}, bf16[2,1024,1024]{1,2,0:T(8,128)(2,1)}, u32[]{:S(2)}, u32[]{:S(2)}) collective-permute-start(bf16[2,1024,1024]{1,2,0:T(8,128)(2,1)} %get-tuple-element.776), channel_id=1, source_target_pairs={{0,8},{8,16},{16,24},{1,9},{9,17},{17,25},{2,10},{10,18},{18,26},{... | collective-permute-start | bytes 12582920 | tf_op jit(solution)/shard_map/while/body/eval_jaxpr/ppermute | solution.py:86
  1139.0 51.2 %collective-permute-done = bf16[2,1024,1024]{1,2,0:T(8,128)(2,1)} collective-permute-done((bf16[2,1024,1024]{1,2,0:T(8,128)(2,1)}, bf16[2,1024,1024]{1,2,0:T(8,128)(2,1)}, u32[]{:S(2)}, u32[]{:S(2)}) %collective-permute-start) | collective-permute-done | bytes 4194336 | tf_op jit(solution)/shard_map/while/body/eval_jaxpr/ppermute | solution.py:86
  1190.2 229.5 %collective-permute-start = (bf16[2,1024,1024]{1,2,0:T(8,128)(2,1)}, bf16[2,1024,1024]{1,2,0:T(8,128)(2,1)}, u32[]{:S(2)}, u32[]{:S(2)}) collective-permute-start(bf16[2,1024,1024]{1,2,0:T(8,128)(2,1)} %get-tuple-element.776), channel_id=1, source_target_pairs={{0,8},{8,16},{16,24},{1,9},{9,17},{17,25},{2,10},{10,18},{18,26},{... | collective-permute-start | bytes 12582920 | tf_op jit(solution)/shard_map/while/body/eval_jaxpr/ppermute | solution.py:86
  1419.7 41.5 %collective-permute-start.1 = (f32[2,32,128,64]{2,3,1,0:T(8,128)}, f32[2,32,128,64]{2,3,1,0:T(8,128)S(1)}, u32[]{:S(2)}, u32[]{:S(2)}) collective-permute-start(f32[2,32,128,64]{2,3,1,0:T(8,128)} %get-tuple-element.777), channel_id=1, source_target_pairs={{0,1},{1,2},{2,3},{3,4},{4,5},{5,6},{6,7},{8,9},{9,10},{10,11},{11... | collective-permute-start | bytes 6291464 | tf_op jit(solution)/shard_map/while/body/eval_jaxpr/ppermute | solution.py:87
  1461.2 3.6 collective-permute-done.1
  1464.8 5.1 collective-permute-done
  1470.0 98.9 %collective-permute-start = (bf16[2,1024,1024]{1,2,0:T(8,128)(2,1)}, bf16[2,1024,1024]{1,2,0:T(8,128)(2,1)}, u32[]{:S(2)}, u32[]{:S(2)}) collective-permute-start(bf16[2,1024,1024]{1,2,0:T(8,128)(2,1)} %get-tuple-element.776), channel_id=1, source_target_pairs={{0,8},{8,16},{16,24},{1,9},{9,17},{17,25},{2,10},{10,18},{18,26},{... | collective-permute-start | bytes 12582920 | tf_op jit(solution)/shard_map/while/body/eval_jaxpr/ppermute | solution.py:86
  1568.9 217.4 %collective-permute-start.1 = (f32[2,32,128,64]{2,3,1,0:T(8,128)}, f32[2,32,128,64]{2,3,1,0:T(8,128)S(1)}, u32[]{:S(2)}, u32[]{:S(2)}) collective-permute-start(f32[2,32,128,64]{2,3,1,0:T(8,128)} %get-tuple-element.777), channel_id=1, source_target_pairs={{0,1},{1,2},{2,3},{3,4},{4,5},{5,6},{6,7},{8,9},{9,10},{10,11},{11... | collective-permute-start | bytes 6291464 | tf_op jit(solution)/shard_map/while/body/eval_jaxpr/ppermute | solution.py:87
  1789.9 88.2 %collective-permute-start = (bf16[2,1024,1024]{1,2,0:T(8,128)(2,1)}, bf16[2,1024,1024]{1,2,0:T(8,128)(2,1)}, u32[]{:S(2)}, u32[]{:S(2)}) collective-permute-start(bf16[2,1024,1024]{1,2,0:T(8,128)(2,1)} %get-tuple-element.776), channel_id=1, source_target_pairs={{0,8},{8,16},{16,24},{1,9},{9,17},{17,25},{2,10},{10,18},{18,26},{... | collective-permute-start | bytes 12582920 | tf_op jit(solution)/shard_map/while/body/eval_jaxpr/ppermute | solution.py:86
  1878.1 67.0 %collective-permute-start.1 = (f32[2,32,128,64]{2,3,1,0:T(8,128)}, f32[2,32,128,64]{2,3,1,0:T(8,128)S(1)}, u32[]{:S(2)}, u32[]{:S(2)}) collective-permute-start(f32[2,32,128,64]{2,3,1,0:T(8,128)} %get-tuple-element.777), channel_id=1, source_target_pairs={{0,1},{1,2},{2,3},{3,4},{4,5},{5,6},{6,7},{8,9},{9,10},{10,11},{11... | collective-permute-start | bytes 6291464 | tf_op jit(solution)/shard_map/while/body/eval_jaxpr/ppermute | solution.py:87
  1948.7 217.3 %collective-permute-start = (bf16[2,1024,1024]{1,2,0:T(8,128)(2,1)}, bf16[2,1024,1024]{1,2,0:T(8,128)(2,1)}, u32[]{:S(2)}, u32[]{:S(2)}) collective-permute-start(bf16[2,1024,1024]{1,2,0:T(8,128)(2,1)} %get-tuple-element.776), channel_id=1, source_target_pairs={{0,8},{8,16},{16,24},{1,9},{9,17},{17,25},{2,10},{10,18},{18,26},{... | collective-permute-start | bytes 12582920 | tf_op jit(solution)/shard_map/while/body/eval_jaxpr/ppermute | solution.py:86
  2166.0 77.8 %collective-permute-start.1 = (f32[2,32,128,64]{2,3,1,0:T(8,128)}, f32[2,32,128,64]{2,3,1,0:T(8,128)S(1)}, u32[]{:S(2)}, u32[]{:S(2)}) collective-permute-start(f32[2,32,128,64]{2,3,1,0:T(8,128)} %get-tuple-element.777), channel_id=1, source_target_pairs={{0,1},{1,2},{2,3},{3,4},{4,5},{5,6},{6,7},{8,9},{9,10},{10,11},{11... | collective-permute-start | bytes 6291464 | tf_op jit(solution)/shard_map/while/body/eval_jaxpr/ppermute | solution.py:87
  2243.8 3.6 collective-permute-done.1
  2247.4 7.0 collective-permute-start
  2254.4 236.8 %collective-permute-start.1 = (f32[2,32,128,64]{2,3,1,0:T(8,128)}, f32[2,32,128,64]{2,3,1,0:T(8,128)S(1)}, u32[]{:S(2)}, u32[]{:S(2)}) collective-permute-start(f32[2,32,128,64]{2,3,1,0:T(8,128)} %get-tuple-element.777), channel_id=1, source_target_pairs={{0,1},{1,2},{2,3},{3,4},{4,5},{5,6},{6,7},{8,9},{9,10},{10,11},{11... | collective-permute-start | bytes 6291464 | tf_op jit(solution)/shard_map/while/body/eval_jaxpr/ppermute | solution.py:87
  2491.2 3.6 collective-permute-done.1
  2498.1 87.8 %collective-permute-start.1 = (f32[2,32,128,64]{2,3,1,0:T(8,128)}, f32[2,32,128,64]{2,3,1,0:T(8,128)S(1)}, u32[]{:S(2)}, u32[]{:S(2)}) collective-permute-start(f32[2,32,128,64]{2,3,1,0:T(8,128)} %get-tuple-element.777), channel_id=1, source_target_pairs={{0,1},{1,2},{2,3},{3,4},{4,5},{5,6},{6,7},{8,9},{9,10},{10,11},{11... | collective-permute-start | bytes 6291464 | tf_op jit(solution)/shard_map/while/body/eval_jaxpr/ppermute | solution.py:87
  2585.9 3.6 collective-permute-done.1
  2592.9 271.5 %collective-permute-start.1 = (f32[2,32,128,64]{2,3,1,0:T(8,128)}, f32[2,32,128,64]{2,3,1,0:T(8,128)S(1)}, u32[]{:S(2)}, u32[]{:S(2)}) collective-permute-start(f32[2,32,128,64]{2,3,1,0:T(8,128)} %get-tuple-element.777), channel_id=1, source_target_pairs={{0,1},{1,2},{2,3},{3,4},{4,5},{5,6},{6,7},{8,9},{9,10},{10,11},{11... | collective-permute-start | bytes 6291464 | tf_op jit(solution)/shard_map/while/body/eval_jaxpr/ppermute | solution.py:87
  2864.3 3.6 collective-permute-done.1
  2871.1 6.2 copy.82
  2877.3 1018.5 %all-reduce.2.cloned.1.call-done = f32[1,2,32,128,64]{3,4,2,1,0:T(8,128)} async-done(((f32[1,2,32,128,64]{3,4,2,1,0:T(8,128)}), f32[1,2,32,128,64]{3,4,2,1,0:T(8,128)}) %all-reduce.2.cloned.1.call-update) | async-done | bytes 2097168 | tf_op jit(solution)/shard_map/psum | solution.py:94
  (66 shorter events, 48.7 us)
Async XLA Ops:
  7.2 3888.6 %all-reduce.2.cloned.1.call-start = ((), (), s32[]{:S(2)}) async-start(), calls=%async_computation | async-start | bytes 4194304 | tf_op jit(solution)/shard_map/psum | solution.py:94
  36.8 1.9 copy-start
  87.3 25.8 copy-start.2
  165.4 99.3 %copy-start.5 = (f32[64]{0:T(128)S(1)}, f32[64]{0:T(128)}, u32[]{:S(2)}) copy-start(f32[64]{0:T(128)} %convert_element_type.40) | copy-start | bytes 772 | tf_op jit(solution)/shard_map/while/body/eval_jaxpr/cond
  264.7 9.1 copy-start.1
  264.7 9.1 copy-start.3
  273.7 11.3 copy-start.4
  345.3 47.3 %collective-permute-start = (bf16[2,1024,1024]{1,2,0:T(8,128)(2,1)}, bf16[2,1024,1024]{1,2,0:T(8,128)(2,1)}, u32[]{:S(2)}, u32[]{:S(2)}) collective-permute-start(bf16[2,1024,1024]{1,2,0:T(8,128)(2,1)} %get-tuple-element.776), channel_id=1, source_target_pairs={{0,8},{8,16},{16,24},{1,9},{9,17},{17,25},{2,10},{10,18},{18,26},{... | collective-permute-start | bytes 12582920 | tf_op jit(solution)/shard_map/while/body/eval_jaxpr/ppermute | solution.py:86
  348.6 5.1 collective-permute-start.1
  401.1 360.5 %collective-permute-start = (bf16[2,1024,1024]{1,2,0:T(8,128)(2,1)}, bf16[2,1024,1024]{1,2,0:T(8,128)(2,1)}, u32[]{:S(2)}, u32[]{:S(2)}) collective-permute-start(bf16[2,1024,1024]{1,2,0:T(8,128)(2,1)} %get-tuple-element.776), channel_id=1, source_target_pairs={{0,8},{8,16},{16,24},{1,9},{9,17},{17,25},{2,10},{10,18},{18,26},{... | collective-permute-start | bytes 12582920 | tf_op jit(solution)/shard_map/while/body/eval_jaxpr/ppermute | solution.py:86
  715.0 5.1 collective-permute-start.1
  761.6 285.6 %collective-permute-start = (bf16[2,1024,1024]{1,2,0:T(8,128)(2,1)}, bf16[2,1024,1024]{1,2,0:T(8,128)(2,1)}, u32[]{:S(2)}, u32[]{:S(2)}) collective-permute-start(bf16[2,1024,1024]{1,2,0:T(8,128)(2,1)} %get-tuple-element.776), channel_id=1, source_target_pairs={{0,8},{8,16},{16,24},{1,9},{9,17},{17,25},{2,10},{10,18},{18,26},{... | collective-permute-start | bytes 12582920 | tf_op jit(solution)/shard_map/while/body/eval_jaxpr/ppermute | solution.py:86
  776.5 270.7 %collective-permute-start.1 = (f32[2,32,128,64]{2,3,1,0:T(8,128)}, f32[2,32,128,64]{2,3,1,0:T(8,128)S(1)}, u32[]{:S(2)}, u32[]{:S(2)}) collective-permute-start(f32[2,32,128,64]{2,3,1,0:T(8,128)} %get-tuple-element.777), channel_id=1, source_target_pairs={{0,1},{1,2},{2,3},{3,4},{4,5},{5,6},{6,7},{8,9},{9,10},{10,11},{11... | collective-permute-start | bytes 6291464 | tf_op jit(solution)/shard_map/while/body/eval_jaxpr/ppermute | solution.py:87
  1047.2 143.0 %collective-permute-start = (bf16[2,1024,1024]{1,2,0:T(8,128)(2,1)}, bf16[2,1024,1024]{1,2,0:T(8,128)(2,1)}, u32[]{:S(2)}, u32[]{:S(2)}) collective-permute-start(bf16[2,1024,1024]{1,2,0:T(8,128)(2,1)} %get-tuple-element.776), channel_id=1, source_target_pairs={{0,8},{8,16},{16,24},{1,9},{9,17},{17,25},{2,10},{10,18},{18,26},{... | collective-permute-start | bytes 12582920 | tf_op jit(solution)/shard_map/while/body/eval_jaxpr/ppermute | solution.py:86
  1134.0 5.1 collective-permute-start.1
  1190.2 279.7 %collective-permute-start = (bf16[2,1024,1024]{1,2,0:T(8,128)(2,1)}, bf16[2,1024,1024]{1,2,0:T(8,128)(2,1)}, u32[]{:S(2)}, u32[]{:S(2)}) collective-permute-start(bf16[2,1024,1024]{1,2,0:T(8,128)(2,1)} %get-tuple-element.776), channel_id=1, source_target_pairs={{0,8},{8,16},{16,24},{1,9},{9,17},{17,25},{2,10},{10,18},{18,26},{... | collective-permute-start | bytes 12582920 | tf_op jit(solution)/shard_map/while/body/eval_jaxpr/ppermute | solution.py:86
  1419.7 45.1 %collective-permute-start.1 = (f32[2,32,128,64]{2,3,1,0:T(8,128)}, f32[2,32,128,64]{2,3,1,0:T(8,128)S(1)}, u32[]{:S(2)}, u32[]{:S(2)}) collective-permute-start(f32[2,32,128,64]{2,3,1,0:T(8,128)} %get-tuple-element.777), channel_id=1, source_target_pairs={{0,1},{1,2},{2,3},{3,4},{4,5},{5,6},{6,7},{8,9},{9,10},{10,11},{11... | collective-permute-start | bytes 6291464 | tf_op jit(solution)/shard_map/while/body/eval_jaxpr/ppermute | solution.py:87
  1470.0 320.0 %collective-permute-start = (bf16[2,1024,1024]{1,2,0:T(8,128)(2,1)}, bf16[2,1024,1024]{1,2,0:T(8,128)(2,1)}, u32[]{:S(2)}, u32[]{:S(2)}) collective-permute-start(bf16[2,1024,1024]{1,2,0:T(8,128)(2,1)} %get-tuple-element.776), channel_id=1, source_target_pairs={{0,8},{8,16},{16,24},{1,9},{9,17},{17,25},{2,10},{10,18},{18,26},{... | collective-permute-start | bytes 12582920 | tf_op jit(solution)/shard_map/while/body/eval_jaxpr/ppermute | solution.py:86
  1568.9 221.1 %collective-permute-start.1 = (f32[2,32,128,64]{2,3,1,0:T(8,128)}, f32[2,32,128,64]{2,3,1,0:T(8,128)S(1)}, u32[]{:S(2)}, u32[]{:S(2)}) collective-permute-start(f32[2,32,128,64]{2,3,1,0:T(8,128)} %get-tuple-element.777), channel_id=1, source_target_pairs={{0,1},{1,2},{2,3},{3,4},{4,5},{5,6},{6,7},{8,9},{9,10},{10,11},{11... | collective-permute-start | bytes 6291464 | tf_op jit(solution)/shard_map/while/body/eval_jaxpr/ppermute | solution.py:87
  1789.9 158.8 %collective-permute-start = (bf16[2,1024,1024]{1,2,0:T(8,128)(2,1)}, bf16[2,1024,1024]{1,2,0:T(8,128)(2,1)}, u32[]{:S(2)}, u32[]{:S(2)}) collective-permute-start(bf16[2,1024,1024]{1,2,0:T(8,128)(2,1)} %get-tuple-element.776), channel_id=1, source_target_pairs={{0,8},{8,16},{16,24},{1,9},{9,17},{17,25},{2,10},{10,18},{18,26},{... | collective-permute-start | bytes 12582920 | tf_op jit(solution)/shard_map/while/body/eval_jaxpr/ppermute | solution.py:86
  1878.1 70.6 %collective-permute-start.1 = (f32[2,32,128,64]{2,3,1,0:T(8,128)}, f32[2,32,128,64]{2,3,1,0:T(8,128)S(1)}, u32[]{:S(2)}, u32[]{:S(2)}) collective-permute-start(f32[2,32,128,64]{2,3,1,0:T(8,128)} %get-tuple-element.777), channel_id=1, source_target_pairs={{0,1},{1,2},{2,3},{3,4},{4,5},{5,6},{6,7},{8,9},{9,10},{10,11},{11... | collective-permute-start | bytes 6291464 | tf_op jit(solution)/shard_map/while/body/eval_jaxpr/ppermute | solution.py:87
  1948.7 298.7 %collective-permute-start = (bf16[2,1024,1024]{1,2,0:T(8,128)(2,1)}, bf16[2,1024,1024]{1,2,0:T(8,128)(2,1)}, u32[]{:S(2)}, u32[]{:S(2)}) collective-permute-start(bf16[2,1024,1024]{1,2,0:T(8,128)(2,1)} %get-tuple-element.776), channel_id=1, source_target_pairs={{0,8},{8,16},{16,24},{1,9},{9,17},{17,25},{2,10},{10,18},{18,26},{... | collective-permute-start | bytes 12582920 | tf_op jit(solution)/shard_map/while/body/eval_jaxpr/ppermute | solution.py:86
  2166.0 81.4 %collective-permute-start.1 = (f32[2,32,128,64]{2,3,1,0:T(8,128)}, f32[2,32,128,64]{2,3,1,0:T(8,128)S(1)}, u32[]{:S(2)}, u32[]{:S(2)}) collective-permute-start(f32[2,32,128,64]{2,3,1,0:T(8,128)} %get-tuple-element.777), channel_id=1, source_target_pairs={{0,1},{1,2},{2,3},{3,4},{4,5},{5,6},{6,7},{8,9},{9,10},{10,11},{11... | collective-permute-start | bytes 6291464 | tf_op jit(solution)/shard_map/while/body/eval_jaxpr/ppermute | solution.py:87
  2247.4 247.4 %collective-permute-start = (bf16[2,1024,1024]{1,2,0:T(8,128)(2,1)}, bf16[2,1024,1024]{1,2,0:T(8,128)(2,1)}, u32[]{:S(2)}, u32[]{:S(2)}) collective-permute-start(bf16[2,1024,1024]{1,2,0:T(8,128)(2,1)} %get-tuple-element.776), channel_id=1, source_target_pairs={{0,8},{8,16},{16,24},{1,9},{9,17},{17,25},{2,10},{10,18},{18,26},{... | collective-permute-start | bytes 12582920 | tf_op jit(solution)/shard_map/while/body/eval_jaxpr/ppermute | solution.py:86
  2254.4 240.4 %collective-permute-start.1 = (f32[2,32,128,64]{2,3,1,0:T(8,128)}, f32[2,32,128,64]{2,3,1,0:T(8,128)S(1)}, u32[]{:S(2)}, u32[]{:S(2)}) collective-permute-start(f32[2,32,128,64]{2,3,1,0:T(8,128)} %get-tuple-element.777), channel_id=1, source_target_pairs={{0,1},{1,2},{2,3},{3,4},{4,5},{5,6},{6,7},{8,9},{9,10},{10,11},{11... | collective-permute-start | bytes 6291464 | tf_op jit(solution)/shard_map/while/body/eval_jaxpr/ppermute | solution.py:87
  2494.8 94.8 %collective-permute-start = (bf16[2,1024,1024]{1,2,0:T(8,128)(2,1)}, bf16[2,1024,1024]{1,2,0:T(8,128)(2,1)}, u32[]{:S(2)}, u32[]{:S(2)}) collective-permute-start(bf16[2,1024,1024]{1,2,0:T(8,128)(2,1)} %get-tuple-element.776), channel_id=1, source_target_pairs={{0,8},{8,16},{16,24},{1,9},{9,17},{17,25},{2,10},{10,18},{18,26},{... | collective-permute-start | bytes 12582920 | tf_op jit(solution)/shard_map/while/body/eval_jaxpr/ppermute | solution.py:86
  2498.1 91.5 %collective-permute-start.1 = (f32[2,32,128,64]{2,3,1,0:T(8,128)}, f32[2,32,128,64]{2,3,1,0:T(8,128)S(1)}, u32[]{:S(2)}, u32[]{:S(2)}) collective-permute-start(f32[2,32,128,64]{2,3,1,0:T(8,128)} %get-tuple-element.777), channel_id=1, source_target_pairs={{0,1},{1,2},{2,3},{3,4},{4,5},{5,6},{6,7},{8,9},{9,10},{10,11},{11... | collective-permute-start | bytes 6291464 | tf_op jit(solution)/shard_map/while/body/eval_jaxpr/ppermute | solution.py:87
  2589.6 278.4 %collective-permute-start = (bf16[2,1024,1024]{1,2,0:T(8,128)(2,1)}, bf16[2,1024,1024]{1,2,0:T(8,128)(2,1)}, u32[]{:S(2)}, u32[]{:S(2)}) collective-permute-start(bf16[2,1024,1024]{1,2,0:T(8,128)(2,1)} %get-tuple-element.776), channel_id=1, source_target_pairs={{0,8},{8,16},{16,24},{1,9},{9,17},{17,25},{2,10},{10,18},{18,26},{... | collective-permute-start | bytes 12582920 | tf_op jit(solution)/shard_map/while/body/eval_jaxpr/ppermute | solution.py:86
  2592.9 275.1 %collective-permute-start.1 = (f32[2,32,128,64]{2,3,1,0:T(8,128)}, f32[2,32,128,64]{2,3,1,0:T(8,128)S(1)}, u32[]{:S(2)}, u32[]{:S(2)}) collective-permute-start(f32[2,32,128,64]{2,3,1,0:T(8,128)} %get-tuple-element.777), channel_id=1, source_target_pairs={{0,1},{1,2},{2,3},{3,4},{4,5},{5,6},{6,7},{8,9},{9,10},{10,11},{11... | collective-permute-start | bytes 6291464 | tf_op jit(solution)/shard_map/while/body/eval_jaxpr/ppermute | solution.py:87
Sparse Core Ops, SparseCore 0:
  2871.2 1024.5 all-reduce.1
where the time goes:
time: 3910 us
  starting transfers between devices  2340 us (60%)
  waiting for transfers between devices  1200 us (31%)
  matrix products  265 us (7%)
  local copies, waits for them, and re-layouts  43.2 us (1%)
  other arithmetic  40.2 us (1%)
    ppermute x11, starting transfers between devices, step_body(): s_recv = lax.ppermute(s_done, 'seq', seq_pairs)  1270 us
    ppermute x11, starting transfers between devices, step_body(): h_recv = lax.ppermute(y_done, 'stage', stage_pairs)  1070 us
    psum x1, waiting for transfers between devices, device_program(): s_final = lax.psum(jnp.where(seq_idx == num_shards - 1, s_done, 0.0), 'seq')  1020 us
    ppermute x11, waiting for transfers between devices, step_body(): h_recv = lax.ppermute(y_done, 'stage', stage_pairs)  137 us
    dot_general x1, matrix products, local_part(): jnp.einsum('bhcj,bjhv->bchv', scores * decay_mat, v_all, preferred_elemen...  99.2 us
  transfers between devices with their start and end apart: 23, of which 16 were waited for; matrix products, arithmetic and copies ran while one was open for 0% of the time, Pallas kernels for 0%

commit v1 on v0

v1 whole, which is shorter than its diff:
```python
import functools

import jax
import jax.numpy as jnp
from jax import lax
from jax.experimental import pallas as pl
from jax.experimental.pallas import tpu as pltpu
from jax.sharding import PartitionSpec as P

NORM_EPS = 1e-6
CHUNK = 256
PAIRS = 4
PIECES = 2
COLS = 256
ROWS = 256
HIDDEN = 512
LINKS = 8


def rms_norm(values, gain_vec):
    mean_sq = jnp.mean(values * values, axis=-1, keepdims=True)
    return values * lax.rsqrt(mean_sq + NORM_EPS) * gain_vec.astype(jnp.float32)


def dot_f32(lhs, rhs):
    return jnp.dot(lhs, rhs, preferred_element_type=jnp.float32)


def project_kernel(key_dim, chunk, h_ref, norm_ref, wg_ref, bias_ref, tri_ref, wq_ref, wk_ref, wv_ref, sin_ref,
                   q_ref, kt_ref, v_ref, cum_ref, sout_ref, u_scr, cum_scr):
    rows = h_ref.shape[0]
    heads = cum_ref.shape[0]
    group = pl.program_id(0)

    @pl.when(group == 0)
    def _():
        u_scr[...] = rms_norm(h_ref[...].astype(jnp.float32), norm_ref[...]).astype(jnp.bfloat16)
        gate = lax.dot_general(wg_ref[...], u_scr[...], (((1,), (1,)), ((), ())), preferred_element_type=jnp.float32)
        log_decay = jax.nn.log_sigmoid(gate + bias_ref[...])
        for start in range(0, rows, chunk):
            cum_scr[:, start:start + chunk] = jnp.dot(
                log_decay[:, start:start + chunk], tri_ref[...], precision=lax.Precision.HIGHEST,
                preferred_element_type=jnp.float32)

    u_norm = u_scr[...]
    for start in range(0, wv_ref.shape[1], COLS):
        v_ref[:, start:start + COLS] = dot_f32(u_norm, wv_ref[:, start:start + COLS]).astype(jnp.bfloat16)
    for start in range(0, wk_ref.shape[1], COLS):
        k_part = dot_f32(u_norm, wk_ref[:, start:start + COLS]) * key_dim ** -0.5
        kt_ref[start:start + COLS, :] = k_part.T.astype(jnp.bfloat16)
    for start in range(0, wq_ref.shape[1], COLS):
        q_ref[:, start:start + COLS] = dot_f32(u_norm, wq_ref[:, start:start + COLS]).astype(jnp.bfloat16)

    cum = cum_scr[pl.ds(pl.multiple_of(group * heads, heads), heads), :]
    cum_ref[...] = cum
    total = jnp.zeros((heads, 1), jnp.float32)
    rest = []
    for start in range(rows - chunk, -1, -chunk):
        last = cum[:, start + chunk - 1:start + chunk]
        rest.insert(0, total + (last - cum[:, start:start + chunk]))
        total = total + last
    weight = jnp.exp(jnp.concatenate(rest, axis=1))
    total = jnp.exp(total)
    wide = sout_ref.shape[2]
    low = lax.broadcasted_iota(jnp.int32, (key_dim, wide), 1) < wide // 2
    for pair in range(sout_ref.shape[0]):
        v_pair = v_ref[:, pair * wide:(pair + 1) * wide]
        state = sin_ref[pair]
        parts = []
        for head in (2 * pair, 2 * pair + 1):
            k_t = kt_ref[head * key_dim:(head + 1) * key_dim, :].astype(jnp.float32)
            parts.append(total[head:head + 1] * state + dot_f32((k_t * weight[head:head + 1]).astype(jnp.bfloat16), v_pair))
        sout_ref[pair] = jnp.where(low, parts[0], parts[1])


def finish_kernel(h_ref, norm_ref, hn_ref, wo_ref, w1_ref, w2_ref, out_ref, acc_scr, in_scr):
    step = pl.program_id(0)
    rows = h_ref.shape[0]

    @pl.when(step == 0)
    def _():
        for start in range(0, h_ref.shape[1], COLS):
            cols = slice(start, start + COLS)
            acc_scr[:, cols] = h_ref[:, cols].astype(jnp.float32) + dot_f32(hn_ref[...], wo_ref[:, cols])
        in_scr[...] = rms_norm(acc_scr[...], norm_ref[...]).astype(jnp.bfloat16)

    for start in range(0, rows, ROWS):
        part = slice(start, start + ROWS)
        hidden = jax.nn.gelu(dot_f32(in_scr[part, :], w1_ref[...]), approximate=True).astype(jnp.bfloat16)
        acc_scr[part, :] += dot_f32(hidden, w2_ref[...])

    @pl.when(step == pl.num_programs(0) - 1)
    def _():
        out_ref[...] = acc_scr[...].astype(jnp.bfloat16)


def attn_kernel(key_dim, q_ref, kt_ref, v_ref, cum_ref, gain_ref, sin_ref, out_ref, sout_ref):
    @pl.when(pl.program_id(1) == 0)
    def _():
        sout_ref[...] = sin_ref[...]

    cum = cum_ref[...]
    chunk = cum.shape[1]
    cum_col = cum.T
    total = cum[:, chunk - 1:]
    wide = sout_ref.shape[2]
    val_dim = wide // 2
    causal = lax.broadcasted_iota(jnp.int32, (chunk, chunk), 0) >= lax.broadcasted_iota(jnp.int32, (chunk, chunk), 1)
    low = lax.broadcasted_iota(jnp.int32, (chunk, wide), 1) < val_dim
    low_s = lax.broadcasted_iota(jnp.int32, (key_dim, wide), 1) < val_dim
    for pair in range(sout_ref.shape[0]):
        v_pair = v_ref[:, pair * wide:(pair + 1) * wide]
        state = sout_ref[pair]
        state_b = state.astype(jnp.bfloat16)
        outs, states = [], []
        for head in (2 * pair, 2 * pair + 1):
            q_head = q_ref[:, head * key_dim:(head + 1) * key_dim]
            k_t = kt_ref[head * key_dim:(head + 1) * key_dim, :]
            row, col = cum_col[:, head:head + 1], cum[head:head + 1]
            decay = jnp.exp(jnp.where(causal, row - col, -jnp.inf))
            weights = (dot_f32(q_head, k_t) * decay).astype(jnp.bfloat16)
            outs.append(dot_f32(weights, v_pair) + dot_f32(q_head, state_b) * jnp.exp(row))
            k_dec = (k_t.astype(jnp.float32) * jnp.exp(total[head:head + 1] - col)).astype(jnp.bfloat16)
            states.append(jnp.exp(total[head:head + 1]) * state + dot_f32(k_dec, v_pair))
        sout_ref[pair] = jnp.where(low_s, states[0], states[1])
        out = jnp.where(low, outs[0], outs[1])
        square = out * out
        low_ms = jnp.sum(jnp.where(low, square, 0.0), axis=1, keepdims=True) * (1.0 / val_dim)
        high_ms = jnp.sum(jnp.where(low, 0.0, square), axis=1, keepdims=True) * (1.0 / val_dim)
        scale = jnp.where(low, lax.rsqrt(low_ms + NORM_EPS), lax.rsqrt(high_ms + NORM_EPS))
        out_ref[:, pair * wide:(pair + 1) * wide] = (out * scale * gain_ref[...]).astype(jnp.bfloat16)


def chain_kernel(n, local_ref, decay_ref, in_ref, out_ref, held, send_sem, recv_sem):
    me = lax.axis_index('seq')
    barrier = pltpu.get_barrier_semaphore()
    groups = send_sem.shape[0]
    size = local_ref.shape[0] // groups

    def copy(group):
        part = pl.ds(group * size, size)
        return pltpu.make_async_remote_copy(
            src_ref=out_ref.at[part], dst_ref=held.at[part],
            send_sem=send_sem.at[group], recv_sem=recv_sem.at[group],
            device_id={'seq': me + 1}, device_id_type=pl.DeviceIdType.MESH)

    @pl.when(me > 0)
    def _():
        pl.semaphore_signal(barrier, inc=1, device_id={'seq': me - 1}, device_id_type=pl.DeviceIdType.MESH)

    @pl.when(me < n - 1)
    def _():
        pl.semaphore_wait(barrier, 1)

    @pl.when(me == 0)
    def _():
        held[...] = jnp.zeros_like(held)

    for group in range(groups):
        part = pl.ds(group * size, size)

        @pl.when(me > 0)
        def _():
            copy(group).wait_recv()

        out_ref[part] = decay_ref[part] * held[part] + local_ref[part]
        in_ref[part] = held[part]

        @pl.when(me < n - 1)
        def _():
            copy(group).start()

    @pl.when(me < n - 1)
    def _():
        for group in range(groups):
            copy(group).wait_send()


def solution(mesh):
    num_stages = mesh.shape['stage']
    num_shards = mesh.shape['seq']
    stage_pairs = [(src, src + 1) for src in range(num_stages - 1)]
    mat_spec = P('stage', None, None)
    vec_spec = P('stage', None)
    weight_specs = (vec_spec, mat_spec, mat_spec, mat_spec, mat_spec, vec_spec, vec_spec, mat_spec, vec_spec, mat_spec, mat_spec)

    def device_program(x_tokens, norm_attn, w_query, w_key, w_value, w_gate, gate_bias, norm_out, w_out, norm_mlp, w_up, w_down):
        stage_idx = lax.axis_index('stage')
        seq_idx = lax.axis_index('seq')
        stacked = (norm_attn, w_query, w_key, w_value, w_gate, gate_bias, norm_out, w_out, norm_mlp, w_up, w_down)
        norm_attn, w_query, w_key, w_value, w_gate, gate_bias, norm_out, w_out, norm_mlp, w_up, w_down = (w[0] for w in stacked)
        num_seqs, tok_len, width = x_tokens.shape
        num_heads = gate_bias.shape[0]
        key_dim = w_query.shape[1] // num_heads
        val_dim = norm_out.shape[0]
        wide = 2 * val_dim
        num_pairs = num_heads // 2
        groups = num_pairs // PAIRS
        rows = tok_len // PIECES
        chunks = rows // CHUNK
        state_shape = (num_pairs, key_dim, wide)
        gain_wide = jnp.tile(norm_out.astype(jnp.float32), 2)[None]
        tri = (jnp.arange(CHUNK)[:, None] <= jnp.arange(CHUNK)[None, :]).astype(jnp.float32)

        kt_block = pl.BlockSpec((2 * PAIRS * key_dim, CHUNK), lambda g, c: (g, c))
        q_block = pl.BlockSpec((CHUNK, 2 * PAIRS * key_dim), lambda g, c: (c, g))
        v_block = pl.BlockSpec((CHUNK, PAIRS * wide), lambda g, c: (c, g))
        cum_block = pl.BlockSpec((2 * PAIRS, CHUNK), lambda g, c: (g, c))
        state_block = pl.BlockSpec((PAIRS, key_dim, wide), lambda g, c: (g, 0, 0))
        state_out = jax.ShapeDtypeStruct(state_shape, jnp.float32)
        params = pltpu.CompilerParams(dimension_semantics=('arbitrary', 'arbitrary'))
        head_rows = num_heads * rows
        key_width, val_width = num_heads * key_dim, num_heads * val_dim
        ffn_dim = w_up.shape[1]
        bf16_out = lambda *shape: jax.ShapeDtypeStruct(shape, jnp.bfloat16)
        whole = lambda *shape: pl.BlockSpec(shape, lambda g: (0,) * len(shape))

        run_project = pl.pallas_call(
            functools.partial(project_kernel, key_dim, CHUNK), grid=(groups,),
            in_specs=[whole(rows, width), whole(1, width), whole(num_heads, width), whole(num_heads, 1), whole(CHUNK, CHUNK),
                      pl.BlockSpec((width, 2 * PAIRS * key_dim), lambda g: (0, g)),
                      pl.BlockSpec((width, 2 * PAIRS * key_dim), lambda g: (0, g)),
                      pl.BlockSpec((width, PAIRS * wide), lambda g: (0, g)),
                      pl.BlockSpec((PAIRS, key_dim, wide), lambda g: (g, 0, 0))],
            out_specs=(pl.BlockSpec((rows, 2 * PAIRS * key_dim), lambda g: (0, g)),
                       pl.BlockSpec((2 * PAIRS * key_dim, rows), lambda g: (g, 0)),
                       pl.BlockSpec((rows, PAIRS * wide), lambda g: (0, g)),
                       pl.BlockSpec((2 * PAIRS, rows), lambda g: (g, 0)),
                       pl.BlockSpec((PAIRS, key_dim, wide), lambda g: (g, 0, 0))),
            out_shape=(bf16_out(rows, key_width), bf16_out(key_width, rows), bf16_out(rows, val_width),
                       jax.ShapeDtypeStruct((num_heads, rows), jnp.float32), state_out),
            scratch_shapes=[pltpu.VMEM((rows, width), jnp.bfloat16), pltpu.VMEM((num_heads, rows), jnp.float32)],
            compiler_params=pltpu.CompilerParams(dimension_semantics=('arbitrary',)), name='project',
            cost_estimate=pl.CostEstimate(flops=2 * rows * width * (2 * key_width + val_width),
                                          bytes_accessed=2 * width * (2 * key_width + val_width), transcendentals=0))
        run_finish = pl.pallas_call(
            finish_kernel, grid=(ffn_dim // HIDDEN,),
            in_specs=[whole(rows, width), whole(1, width), whole(rows, val_width), whole(val_width, width),
                      pl.BlockSpec((width, HIDDEN), lambda g: (0, g)), pl.BlockSpec((HIDDEN, width), lambda g: (g, 0))],
            out_specs=whole(rows, width), out_shape=bf16_out(rows, width),
            scratch_shapes=[pltpu.VMEM((rows, width), jnp.float32), pltpu.VMEM((rows, width), jnp.bfloat16)],
            compiler_params=pltpu.CompilerParams(dimension_semantics=('arbitrary',)), name='finish',
            cost_estimate=pl.CostEstimate(flops=2 * rows * width * (val_width + 2 * ffn_dim),
                                          bytes_accessed=2 * width * (val_width + 2 * ffn_dim), transcendentals=rows * ffn_dim))
        run_attn = pl.pallas_call(
            functools.partial(attn_kernel, key_dim), grid=(groups, chunks),
            in_specs=[q_block, kt_block, v_block, cum_block, pl.BlockSpec((1, wide), lambda g, c: (0, 0)), state_block],
            out_specs=(v_block, state_block),
            out_shape=(jax.ShapeDtypeStruct((rows, num_heads * val_dim), jnp.bfloat16), state_out),
            compiler_params=params, name='chunk_attention',
            cost_estimate=pl.CostEstimate(flops=2 * head_rows * (CHUNK * (key_dim + wide) + 2 * key_dim * wide),
                                          bytes_accessed=12 * rows * num_heads * val_dim, transcendentals=head_rows * CHUNK))
        run_chain = pl.pallas_call(
            functools.partial(chain_kernel, num_shards),
            in_specs=[pl.BlockSpec(memory_space=pltpu.VMEM)] * 2,
            out_specs=(pl.BlockSpec(memory_space=pltpu.VMEM),) * 2,
            out_shape=(state_out, state_out),
            scratch_shapes=[pltpu.VMEM(state_shape, jnp.float32), pltpu.SemaphoreType.DMA((LINKS,)), pltpu.SemaphoreType.DMA((LINKS,))],
            compiler_params=pltpu.CompilerParams(collective_id=0, has_side_effects=True), name='state_chain')

        norm_attn, norm_mlp = norm_attn[None], norm_mlp[None]
        w_gate, gate_bias = w_gate.T, gate_bias[:, None]

        def run_layer(h_pieces, first):
            state = jnp.zeros(state_shape, jnp.float32)
            proj, totals = [], []
            for piece, h_in in enumerate(h_pieces):
                if first is not None:
                    h_in, state = lax.optimization_barrier((h_in, state))
                    h_in = h_pieces[piece] = jnp.where(stage_idx == 0, first[piece], h_in)
                *parts, state = run_project(h_in, norm_attn, w_gate, gate_bias, tri, w_query, w_key, w_value, state)
                proj.append(parts)
                totals.append(jnp.sum(parts[3][:, CHUNK - 1::CHUNK], axis=1))
            decay = jnp.repeat(jnp.exp(sum(totals)).reshape(num_pairs, 1, 2), val_dim, axis=2)
            state, state_last = run_chain(state, decay)
            h_out = []
            for h_in, (q_all, k_t, v_all, cum) in zip(h_pieces, proj):
                head_norm, state = run_attn(q_all, k_t, v_all, cum, gain_wide, state)
                h_out.append(run_finish(h_in, norm_mlp, head_norm, w_out, w_up, w_down))
            return h_out, state_last

        h_ticks, s_ticks = [], []
        h_recv = None
        for tick in range(num_stages + num_seqs - 1):
            first = None
            if tick < num_seqs:
                first = [x_tokens[tick, piece * rows:(piece + 1) * rows] for piece in range(PIECES)]
            if h_recv is None:
                h_recv, first = first, None
            h_out, state_last = run_layer(h_recv, first)
            h_ticks.append(h_out)
            s_ticks.append(state_last)
            if tick < num_stages + num_seqs - 2:
                h_recv = [lax.ppermute(a, 'stage', stage_pairs) for a in h_out]
        s_out = jnp.stack([lax.select_n(stage_idx, *s_ticks[seq:seq + num_stages]) for seq in range(num_seqs)])
        s_out = lax.psum(jnp.where(seq_idx == num_shards - 1, s_out, 0.0), 'seq')
        y_out = jnp.stack([
            jnp.concatenate([lax.select_n(stage_idx, *[h_ticks[seq + stage][piece] for stage in range(num_stages)])
                             for piece in range(PIECES)], axis=0) for seq in range(num_seqs)])
        s_out = s_out.reshape(num_seqs, num_pairs, key_dim, 2, val_dim)
        s_out = jnp.swapaxes(s_out, 2, 3).reshape(num_seqs, num_heads, key_dim, val_dim)
        return y_out[None], s_out[None]

    return jax.shard_map(
        device_program,
        mesh=mesh,
        in_specs=(P('batch', 'seq', None),) + weight_specs,
        out_specs=(P('stage', 'batch', 'seq', None), P('stage', 'batch', None, None, None)),
        check_vma=False,
    )
```

time: 3910 us -> 754 us (0.19)
  the two profiles are of different devices: /device:TPU:96 before, /device:TPU:111 now
where the time goes in v1:
time: 754 us; the launch traced here: 746 us
  Pallas kernels  653 us (87%)
  local copies, waits for them, and re-layouts  30.1 us (4%)
  starting transfers between devices  21.2 us (3%)
  between operations  14.8 us (2%)
  other arithmetic  14.6 us (2%)
  waiting for transfers between devices  12.5 us (2%)
    pallas_call x10, Pallas kernels, run_layer(): h_out.append(run_finish(h_in, norm_mlp, head_norm, w_out, w_up, w_down))  202 us
    pallas_call x10, Pallas kernels, run_layer(): run_project(h_in, norm_attn, w_gate, gate_bias, tri, w_query, w_key, w_va...  187 us
    pallas_call x10, Pallas kernels, run_layer(): head_norm, state = run_attn(q_all, k_t, v_all, cum, gain_wide, state)  160 us
    pallas_call x5, Pallas kernels, run_layer(): state, state_last = run_chain(state, decay)  104 us
    ppermute x8, starting transfers between devices, device_program(): h_recv = [lax.ppermute(a, 'stage', stage_pairs) for a in h_out]  21.2 us
  transfers between devices with their start and end apart: 9, of which 4 were waited for; matrix products, arithmetic and copies ran while one was open for 1% of the time, Pallas kernels for 39%

profile of v1, /device:TPU:111, one launch (start us, length us, event | category | flops | bytes accessed | tf_op | source)
XLA Modules:
  0.0 746.1 jit_solution(5041115545617595675)
XLA Ops:
  10.5 3.0 slice_bitcast_fusion.1
  14.7 18.6 %project.10 = (bf16[512,4096]{1,0:T(8,128)(2,1)}, bf16[4096,512]{1,0:T(8,128)(2,1)}, bf16[512,2048]{1,0:T(8,128)(2,1)}, f32[32,512]{1,0:T(8,128)}, f32[16,128,128]{2,1,0:T(8,128)}) custom-call(bf16[512,1024]{1,0:T(8,128)(2,1)} %get-tuple-element.160.h_ref, bf16[1,1024]{1,0:T(2,128)(2,1)} %norm_ref.37, bf16[32,1024]{1,0:T(8,128)(2,1)} %bitcast.98, ...), custom_call_target="tpu_custom_call" | custom-call | flops 10737418240 | bytes 20971520 | tf_op jit(solution)/shard_map/project/pallas_call | solution.py:271
  34.3 18.7 %project.11 = (bf16[512,4096]{1,0:T(8,128)(2,1)}, bf16[4096,512]{1,0:T(8,128)(2,1)}, bf16[512,2048]{1,0:T(8,128)(2,1)}, f32[32,512]{1,0:T(8,128)}, f32[16,128,128]{2,1,0:T(8,128)}) custom-call(bf16[512,1024]{1,0:T(8,128)(2,1)} %get-tuple-element.161.h_ref, bf16[1,1024]{1,0:T(2,128)(2,1)} %norm_ref.37, bf16[32,1024]{1,0:T(8,128)(2,1)} %bitcast.99, ...), custom_call_target="tpu_custom_call" | custom-call | flops 10737418240 | bytes 20971520 | tf_op jit(solution)/shard_map/project/pallas_call | solution.py:271
  54.9 27.3 %state_chain.5 = (f32[16,128,128]{2,1,0:T(8,128)}, f32[16,128,128]{2,1,0:T(8,128)}) custom-call(f32[16,128,128]{2,1,0:T(8,128)} %get-tuple-element.86.local_ref, f32[16,1,128]{2,1,0:T(1,128)} %broadcast_in_dim.35.decay_ref), custom_call_target="tpu_custom_call" | custom-call | tf_op jit(solution)/shard_map/state_chain/pallas_call | solution.py:275
  82.2 16.0 %chunk_attention.10 = (bf16[512,2048]{1,0:T(8,128)(2,1)}, f32[16,128,128]{2,1,0:T(8,128)}) custom-call(bf16[512,4096]{1,0:T(8,128)(2,1)} %get-tuple-element.81.q_ref, bf16[4096,512]{1,0:T(8,128)(2,1)} %get-tuple-element.82.kt_ref, bf16[512,2048]{1,0:T(8,128)(2,1)} %get-tuple-element.83.v_ref, f32[32,512]{1,0:T(8,128)} %get-tuple-element.84.cum_ref, ...), custom_call_target="tpu_custom_call" | custom-call | flops 3221225472 | bytes 12582912 | tf_op jit(solution)/shard_map/chunk_attention/pallas_call | solution.py:278
  98.2 20.1 %finish.10 = bf16[512,1024]{1,0:T(8,128)(2,1)} custom-call(bf16[512,1024]{1,0:T(8,128)(2,1)} %get-tuple-element.160.h_ref, bf16[1,1024]{1,0:T(2,128)(2,1)} %norm_ref.39, bf16[512,2048]{1,0:T(8,128)(2,1)} %get-tuple-element.89.hn_ref, bf16[2048,1024]{1,0:T(8,128)(2,1)} %bitcast.88, bf16[1024,4096]{1,0:T(8,128)(2,1)} %bitcast.58, bf16[4096,1024]{1,0:T(8,128)(2,1)} %bitcast.68), custom_call_target="tpu_custom_call" | custom-call | flops 10737418240 | bytes 20971520 | tf_op jit(solution)/shard_map/finish/pallas_call | solution.py:279
  118.4 3.8 collective-permute-start
  122.1 16.0 %chunk_attention.11 = (bf16[512,2048]{1,0:T(8,128)(2,1)}, f32[16,128,128]{2,1,0:T(8,128)}) custom-call(bf16[512,4096]{1,0:T(8,128)(2,1)} %get-tuple-element.96.q_ref, bf16[4096,512]{1,0:T(8,128)(2,1)} %get-tuple-element.97.kt_ref, bf16[512,2048]{1,0:T(8,128)(2,1)} %get-tuple-element.98.v_ref, f32[32,512]{1,0:T(8,128)} %get-tuple-element.87.cum_ref, ...), custom_call_target="tpu_custom_call" | custom-call | flops 3221225472 | bytes 12582912 | tf_op jit(solution)/shard_map/chunk_attention/pallas_call | solution.py:278
  138.1 20.2 %finish.11 = bf16[512,1024]{1,0:T(8,128)(2,1)} custom-call(bf16[512,1024]{1,0:T(8,128)(2,1)} %get-tuple-element.161.h_ref, bf16[1,1024]{1,0:T(2,128)(2,1)} %norm_ref.39, bf16[512,2048]{1,0:T(8,128)(2,1)} %get-tuple-element.100.hn_ref, bf16[2048,1024]{1,0:T(8,128)(2,1)} %bitcast.89, bf16[1024,4096]{1,0:T(8,128)(2,1)} %bitcast.59, bf16[4096,1024]{1,0:T(8,128)(2,1)} %bitcast.69), custom_call_target="tpu_custom_call" | custom-call | flops 10737418240 | bytes 20971520 | tf_op jit(solution)/shard_map/finish/pallas_call | solution.py:279
  158.3 3.6 collective-permute-start.1
  162.0 2.4 bitcast_select_fusion.1.h_ref
  164.3 18.6 %project.12 = (bf16[512,4096]{1,0:T(8,128)(2,1)}, bf16[4096,512]{1,0:T(8,128)(2,1)}, bf16[512,2048]{1,0:T(8,128)(2,1)}, f32[32,512]{1,0:T(8,128)}, f32[16,128,128]{2,1,0:T(8,128)}) custom-call(bf16[512,1024]{1,0:T(8,128)(2,1)} %bitcast_select_fusion.1.h_ref, bf16[1,1024]{1,0:T(2,128)(2,1)} %norm_ref.37, bf16[32,1024]{1,0:T(8,128)(2,1)} %bitcast.100, ...), custom_call_target="tpu_custom_call" | custom-call | flops 10737418240 | bytes 20971520 | tf_op jit(solution)/shard_map/project/pallas_call | solution.py:271
  184.5 2.3 bitcast_select_fusion.h_ref
  187.9 18.7 %project.13 = (bf16[512,4096]{1,0:T(8,128)(2,1)}, bf16[4096,512]{1,0:T(8,128)(2,1)}, bf16[512,2048]{1,0:T(8,128)(2,1)}, f32[32,512]{1,0:T(8,128)}, f32[16,128,128]{2,1,0:T(8,128)}) custom-call(bf16[512,1024]{1,0:T(8,128)(2,1)} %bitcast_select_fusion.h_ref, bf16[1,1024]{1,0:T(2,128)(2,1)} %norm_ref.37, bf16[32,1024]{1,0:T(8,128)(2,1)} %bitcast.101, ...), custom_call_target="tpu_custom_call" | custom-call | flops 10737418240 | bytes 20971520 | tf_op jit(solution)/shard_map/project/pallas_call | solution.py:271
  208.4 19.1 %state_chain.6 = (f32[16,128,128]{2,1,0:T(8,128)}, f32[16,128,128]{2,1,0:T(8,128)}) custom-call(f32[16,128,128]{2,1,0:T(8,128)} %get-tuple-element.104.local_ref, f32[16,1,128]{2,1,0:T(1,128)} %broadcast_in_dim.37.decay_ref), custom_call_target="tpu_custom_call" | custom-call | tf_op jit(solution)/shard_map/state_chain/pallas_call | solution.py:275
  227.5 16.0 %chunk_attention.12 = (bf16[512,2048]{1,0:T(8,128)(2,1)}, f32[16,128,128]{2,1,0:T(8,128)}) custom-call(bf16[512,4096]{1,0:T(8,128)(2,1)} %get-tuple-element.92.q_ref, bf16[4096,512]{1,0:T(8,128)(2,1)} %get-tuple-element.93.kt_ref, bf16[512,2048]{1,0:T(8,128)(2,1)} %get-tuple-element.94.v_ref, f32[32,512]{1,0:T(8,128)} %get-tuple-element.95.cum_ref, ...), custom_call_target="tpu_custom_call" | custom-call | flops 3221225472 | bytes 12582912 | tf_op jit(solution)/shard_map/chunk_attention/pallas_call | solution.py:278
  243.5 20.1 %finish.12 = bf16[512,1024]{1,0:T(8,128)(2,1)} custom-call(bf16[512,1024]{1,0:T(8,128)(2,1)} %bitcast_select_fusion.1.h_ref, bf16[1,1024]{1,0:T(2,128)(2,1)} %norm_ref.39, bf16[512,2048]{1,0:T(8,128)(2,1)} %get-tuple-element.107.hn_ref, bf16[2048,1024]{1,0:T(8,128)(2,1)} %bitcast.90, bf16[1024,4096]{1,0:T(8,128)(2,1)} %bitcast.60, bf16[4096,1024]{1,0:T(8,128)(2,1)} %bitcast.70), custom_call_target="tpu_custom_call" | custom-call | flops 10737418240 | bytes 20971520 | tf_op jit(solution)/shard_map/finish/pallas_call | solution.py:279
  263.7 3.7 collective-permute-start.2
  267.4 16.0 %chunk_attention.13 = (bf16[512,2048]{1,0:T(8,128)(2,1)}, f32[16,128,128]{2,1,0:T(8,128)}) custom-call(bf16[512,4096]{1,0:T(8,128)(2,1)} %get-tuple-element.112.q_ref, bf16[4096,512]{1,0:T(8,128)(2,1)} %get-tuple-element.113.kt_ref, bf16[512,2048]{1,0:T(8,128)(2,1)} %get-tuple-element.114.v_ref, f32[32,512]{1,0:T(8,128)} %get-tuple-element.105.cum_ref, ...), custom_call_target="tpu_custom_call" | custom-call | flops 3221225472 | bytes 12582912 | tf_op jit(solution)/shard_map/chunk_attention/pallas_call | solution.py:278
  283.4 20.2 %finish.13 = bf16[512,1024]{1,0:T(8,128)(2,1)} custom-call(bf16[512,1024]{1,0:T(8,128)(2,1)} %bitcast_select_fusion.h_ref, bf16[1,1024]{1,0:T(2,128)(2,1)} %norm_ref.39, bf16[512,2048]{1,0:T(8,128)(2,1)} %get-tuple-element.116.hn_ref, bf16[2048,1024]{1,0:T(8,128)(2,1)} %bitcast.91, bf16[1024,4096]{1,0:T(8,128)(2,1)} %bitcast.61, bf16[4096,1024]{1,0:T(8,128)(2,1)} %bitcast.71), custom_call_target="tpu_custom_call" | custom-call | flops 10737418240 | bytes 20971520 | tf_op jit(solution)/shard_map/finish/pallas_call | solution.py:279
  306.5 18.6 %project.14 = (bf16[512,4096]{1,0:T(8,128)(2,1)}, bf16[4096,512]{1,0:T(8,128)(2,1)}, bf16[512,2048]{1,0:T(8,128)(2,1)}, f32[32,512]{1,0:T(8,128)}, f32[16,128,128]{2,1,0:T(8,128)}) custom-call(bf16[512,1024]{1,0:T(8,128)(2,1)} %copy-done.8, bf16[1,1024]{1,0:T(2,128)(2,1)} %norm_ref.37, bf16[32,1024]{1,0:T(8,128)(2,1)} %bitcast.102, f32[32,1]{1,0:T(8,128)} %copy.25.bias_ref, ...), custom_call_target="tpu_custom_call" | custom-call | flops 10737418240 | bytes 20971520 | tf_op jit(solution)/shard_map/project/pallas_call | solution.py:271
  326.1 3.7 collective-permute-done.3.h_ref
  330.8 18.7 %project.15 = (bf16[512,4096]{1,0:T(8,128)(2,1)}, bf16[4096,512]{1,0:T(8,128)(2,1)}, bf16[512,2048]{1,0:T(8,128)(2,1)}, f32[32,512]{1,0:T(8,128)}, f32[16,128,128]{2,1,0:T(8,128)}) custom-call(bf16[512,1024]{1,0:T(8,128)(2,1)} %copy-done.9, bf16[1,1024]{1,0:T(2,128)(2,1)} %norm_ref.37, bf16[32,1024]{1,0:T(8,128)(2,1)} %bitcast.103, f32[32,1]{1,0:T(8,128)} %copy.25.bias_ref, ...), custom_call_target="tpu_custom_call" | custom-call | flops 10737418240 | bytes 20971520 | tf_op jit(solution)/shard_map/project/pallas_call | solution.py:271
  351.3 19.5 %state_chain.7 = (f32[16,128,128]{2,1,0:T(8,128)}, f32[16,128,128]{2,1,0:T(8,128)}) custom-call(f32[16,128,128]{2,1,0:T(8,128)} %get-tuple-element.118.local_ref, f32[16,1,128]{2,1,0:T(1,128)} %broadcast_in_dim.39.decay_ref), custom_call_target="tpu_custom_call" | custom-call | tf_op jit(solution)/shard_map/state_chain/pallas_call | solution.py:275
  370.8 16.0 %chunk_attention.14 = (bf16[512,2048]{1,0:T(8,128)(2,1)}, f32[16,128,128]{2,1,0:T(8,128)}) custom-call(bf16[512,4096]{1,0:T(8,128)(2,1)} %get-tuple-element.108.q_ref, bf16[4096,512]{1,0:T(8,128)(2,1)} %get-tuple-element.109.kt_ref, bf16[512,2048]{1,0:T(8,128)(2,1)} %get-tuple-element.110.v_ref, f32[32,512]{1,0:T(8,128)} %get-tuple-element.111.cum_ref, ...), custom_call_target="tpu_custom_call" | custom-call | flops 3221225472 | bytes 12582912 | tf_op jit(solution)/shard_map/chunk_attention/pallas_call | solution.py:278
  386.8 20.2 %finish.14 = bf16[512,1024]{1,0:T(8,128)(2,1)} custom-call(bf16[512,1024]{1,0:T(8,128)(2,1)} %copy-done.8, bf16[1,1024]{1,0:T(2,128)(2,1)} %norm_ref.39, bf16[512,2048]{1,0:T(8,128)(2,1)} %get-tuple-element.121.hn_ref, bf16[2048,1024]{1,0:T(8,128)(2,1)} %bitcast.92, bf16[1024,4096]{1,0:T(8,128)(2,1)} %bitcast.62, bf16[4096,1024]{1,0:T(8,128)(2,1)} %bitcast.72), custom_call_target="tpu_custom_call" | custom-call | flops 10737418240 | bytes 20971520 | tf_op jit(solution)/shard_map/finish/pallas_call | solution.py:279
  409.0 16.0 %chunk_attention.15 = (bf16[512,2048]{1,0:T(8,128)(2,1)}, f32[16,128,128]{2,1,0:T(8,128)}) custom-call(bf16[512,4096]{1,0:T(8,128)(2,1)} %get-tuple-element.126.q_ref, bf16[4096,512]{1,0:T(8,128)(2,1)} %get-tuple-element.127.kt_ref, bf16[512,2048]{1,0:T(8,128)(2,1)} %get-tuple-element.128.v_ref, f32[32,512]{1,0:T(8,128)} %get-tuple-element.119.cum_ref, ...), custom_call_target="tpu_custom_call" | custom-call | flops 3221225472 | bytes 12582912 | tf_op jit(solution)/shard_map/chunk_attention/pallas_call | solution.py:278
  425.0 20.1 %finish.15 = bf16[512,1024]{1,0:T(8,128)(2,1)} custom-call(bf16[512,1024]{1,0:T(8,128)(2,1)} %copy-done.9, bf16[1,1024]{1,0:T(2,128)(2,1)} %norm_ref.39, bf16[512,2048]{1,0:T(8,128)(2,1)} %get-tuple-element.130.hn_ref, bf16[2048,1024]{1,0:T(8,128)(2,1)} %bitcast.93, bf16[1024,4096]{1,0:T(8,128)(2,1)} %bitcast.63, bf16[4096,1024]{1,0:T(8,128)(2,1)} %bitcast.73), custom_call_target="tpu_custom_call" | custom-call | flops 10737418240 | bytes 20971520 | tf_op jit(solution)/shard_map/finish/pallas_call | solution.py:279
  448.3 18.6 %project.16 = (bf16[512,4096]{1,0:T(8,128)(2,1)}, bf16[4096,512]{1,0:T(8,128)(2,1)}, bf16[512,2048]{1,0:T(8,128)(2,1)}, f32[32,512]{1,0:T(8,128)}, f32[16,128,128]{2,1,0:T(8,128)}) custom-call(bf16[512,1024]{1,0:T(8,128)(2,1)} %copy-done.10, bf16[1,1024]{1,0:T(2,128)(2,1)} %norm_ref.37, bf16[32,1024]{1,0:T(8,128)(2,1)} %bitcast.104, f32[32,1]{1,0:T(8,128)} %copy.25.bias_ref, ...), custom_call_target="tpu_custom_call" | custom-call | flops 10737418240 | bytes 20971520 | tf_op jit(solution)/shard_map/project/pallas_call | solution.py:271
  467.9 3.5 collective-permute-done.5.h_ref
  472.4 18.7 %project.17 = (bf16[512,4096]{1,0:T(8,128)(2,1)}, bf16[4096,512]{1,0:T(8,128)(2,1)}, bf16[512,2048]{1,0:T(8,128)(2,1)}, f32[32,512]{1,0:T(8,128)}, f32[16,128,128]{2,1,0:T(8,128)}) custom-call(bf16[512,1024]{1,0:T(8,128)(2,1)} %copy-done.11, bf16[1,1024]{1,0:T(2,128)(2,1)} %norm_ref.37, bf16[32,1024]{1,0:T(8,128)(2,1)} %bitcast.105, f32[32,1]{1,0:T(8,128)} %copy.25.bias_ref, ...), custom_call_target="tpu_custom_call" | custom-call | flops 10737418240 | bytes 20971520 | tf_op jit(solution)/shard_map/project/pallas_call | solution.py:271
  492.9 19.1 %state_chain.8 = (f32[16,128,128]{2,1,0:T(8,128)}, f32[16,128,128]{2,1,0:T(8,128)}) custom-call(f32[16,128,128]{2,1,0:T(8,128)} %get-tuple-element.132.local_ref, f32[16,1,128]{2,1,0:T(1,128)} %broadcast_in_dim.41.decay_ref), custom_call_target="tpu_custom_call" | custom-call | tf_op jit(solution)/shard_map/state_chain/pallas_call | solution.py:275
  512.1 16.0 %chunk_attention.16 = (bf16[512,2048]{1,0:T(8,128)(2,1)}, f32[16,128,128]{2,1,0:T(8,128)}) custom-call(bf16[512,4096]{1,0:T(8,128)(2,1)} %get-tuple-element.122.q_ref, bf16[4096,512]{1,0:T(8,128)(2,1)} %get-tuple-element.123.kt_ref, bf16[512,2048]{1,0:T(8,128)(2,1)} %get-tuple-element.124.v_ref, f32[32,512]{1,0:T(8,128)} %get-tuple-element.125.cum_ref, ...), custom_call_target="tpu_custom_call" | custom-call | flops 3221225472 | bytes 12582912 | tf_op jit(solution)/shard_map/chunk_attention/pallas_call | solution.py:278
  528.1 20.1 %finish.16 = bf16[512,1024]{1,0:T(8,128)(2,1)} custom-call(bf16[512,1024]{1,0:T(8,128)(2,1)} %copy-done.10, bf16[1,1024]{1,0:T(2,128)(2,1)} %norm_ref.39, bf16[512,2048]{1,0:T(8,128)(2,1)} %get-tuple-element.135.hn_ref, bf16[2048,1024]{1,0:T(8,128)(2,1)} %bitcast.94, bf16[1024,4096]{1,0:T(8,128)(2,1)} %bitcast.64, bf16[4096,1024]{1,0:T(8,128)(2,1)} %bitcast.74), custom_call_target="tpu_custom_call" | custom-call | flops 10737418240 | bytes 20971520 | tf_op jit(solution)/shard_map/finish/pallas_call | solution.py:279
  548.2 2.2 collective-permute-start.6
  550.4 16.0 %chunk_attention.17 = (bf16[512,2048]{1,0:T(8,128)(2,1)}, f32[16,128,128]{2,1,0:T(8,128)}) custom-call(bf16[512,4096]{1,0:T(8,128)(2,1)} %get-tuple-element.136.q_ref, bf16[4096,512]{1,0:T(8,128)(2,1)} %get-tuple-element.137.kt_ref, bf16[512,2048]{1,0:T(8,128)(2,1)} %get-tuple-element.138.v_ref, f32[32,512]{1,0:T(8,128)} %get-tuple-element.133.cum_ref, ...), custom_call_target="tpu_custom_call" | custom-call | flops 3221225472 | bytes 12582912 | tf_op jit(solution)/shard_map/chunk_attention/pallas_call | solution.py:278
  566.4 20.2 %finish.17 = bf16[512,1024]{1,0:T(8,128)(2,1)} custom-call(bf16[512,1024]{1,0:T(8,128)(2,1)} %copy-done.11, bf16[1,1024]{1,0:T(2,128)(2,1)} %norm_ref.39, bf16[512,2048]{1,0:T(8,128)(2,1)} %get-tuple-element.140.hn_ref, bf16[2048,1024]{1,0:T(8,128)(2,1)} %bitcast.95, bf16[1024,4096]{1,0:T(8,128)(2,1)} %bitcast.65, bf16[4096,1024]{1,0:T(8,128)(2,1)} %bitcast.75), custom_call_target="tpu_custom_call" | custom-call | flops 10737418240 | bytes 20971520 | tf_op jit(solution)/shard_map/finish/pallas_call | solution.py:279
  589.4 18.6 %project.18 = (bf16[512,4096]{1,0:T(8,128)(2,1)}, bf16[4096,512]{1,0:T(8,128)(2,1)}, bf16[512,2048]{1,0:T(8,128)(2,1)}, f32[32,512]{1,0:T(8,128)}, f32[16,128,128]{2,1,0:T(8,128)}) custom-call(bf16[512,1024]{1,0:T(8,128)(2,1)} %copy-done.6, bf16[1,1024]{1,0:T(2,128)(2,1)} %norm_ref.37, bf16[32,1024]{1,0:T(8,128)(2,1)} %bitcast.106, f32[32,1]{1,0:T(8,128)} %copy.25.bias_ref, ...), custom_call_target="tpu_custom_call" | custom-call | flops 10737418240 | bytes 20971520 | tf_op jit(solution)/shard_map/project/pallas_call | solution.py:271
  609.1 3.7 collective-permute-done.7.h_ref
  613.7 18.9 %project.19 = (bf16[512,4096]{1,0:T(8,128)(2,1)}, bf16[4096,512]{1,0:T(8,128)(2,1)}, bf16[512,2048]{1,0:T(8,128)(2,1)}, f32[32,512]{1,0:T(8,128)}, f32[16,128,128]{2,1,0:T(8,128)}) custom-call(bf16[512,1024]{1,0:T(8,128)(2,1)} %copy-done.7, bf16[1,1024]{1,0:T(2,128)(2,1)} %norm_ref.37, bf16[32,1024]{1,0:T(8,128)(2,1)} %bitcast.107, f32[32,1]{1,0:T(8,128)} %copy.25.bias_ref, ...), custom_call_target="tpu_custom_call" | custom-call | flops 10737418240 | bytes 20971520 | tf_op jit(solution)/shard_map/project/pallas_call | solution.py:271
  634.5 19.3 %state_chain.9 = (f32[16,128,128]{2,1,0:T(8,128)}, f32[16,128,128]{2,1,0:T(8,128)}) custom-call(f32[16,128,128]{2,1,0:T(8,128)} %get-tuple-element.146.local_ref, f32[16,1,128]{2,1,0:T(1,128)} %broadcast_in_dim.43.decay_ref), custom_call_target="tpu_custom_call" | custom-call | tf_op jit(solution)/shard_map/state_chain/pallas_call | solution.py:275
  657.7 16.0 %chunk_attention.18 = (bf16[512,2048]{1,0:T(8,128)(2,1)}, f32[16,128,128]{2,1,0:T(8,128)}) custom-call(bf16[512,4096]{1,0:T(8,128)(2,1)} %get-tuple-element.141.q_ref, bf16[4096,512]{1,0:T(8,128)(2,1)} %get-tuple-element.142.kt_ref, bf16[512,2048]{1,0:T(8,128)(2,1)} %get-tuple-element.143.v_ref, f32[32,512]{1,0:T(8,128)} %get-tuple-element.144.cum_ref, ...), custom_call_target="tpu_custom_call" | custom-call | flops 3221225472 | bytes 12582912 | tf_op jit(solution)/shard_map/chunk_attention/pallas_call | solution.py:278
  673.7 16.0 %chunk_attention.19 = (bf16[512,2048]{1,0:T(8,128)(2,1)}, f32[16,128,128]{2,1,0:T(8,128)}) custom-call(bf16[512,4096]{1,0:T(8,128)(2,1)} %get-tuple-element.150.q_ref, bf16[4096,512]{1,0:T(8,128)(2,1)} %get-tuple-element.151.kt_ref, bf16[512,2048]{1,0:T(8,128)(2,1)} %get-tuple-element.152.v_ref, f32[32,512]{1,0:T(8,128)} %get-tuple-element.147.cum_ref, ...), custom_call_target="tpu_custom_call" | custom-call | flops 3221225472 | bytes 12582912 | tf_op jit(solution)/shard_map/chunk_attention/pallas_call | solution.py:278
  689.7 20.1 %finish.19 = bf16[512,1024]{1,0:T(8,128)(2,1)} custom-call(bf16[512,1024]{1,0:T(8,128)(2,1)} %copy-done.7, bf16[1,1024]{1,0:T(2,128)(2,1)} %norm_ref.39, bf16[512,2048]{1,0:T(8,128)(2,1)} %get-tuple-element.154.hn_ref, bf16[2048,1024]{1,0:T(8,128)(2,1)} %bitcast.96, bf16[1024,4096]{1,0:T(8,128)(2,1)} %bitcast.66, bf16[4096,1024]{1,0:T(8,128)(2,1)} %bitcast.76), custom_call_target="tpu_custom_call" | custom-call | flops 10737418240 | bytes 20971520 | tf_op jit(solution)/shard_map/finish/pallas_call | solution.py:279
  709.8 20.3 %finish.18 = bf16[512,1024]{1,0:T(8,128)(2,1)} custom-call(bf16[512,1024]{1,0:T(8,128)(2,1)} %copy-done.6, bf16[1,1024]{1,0:T(2,128)(2,1)} %norm_ref.39, bf16[512,2048]{1,0:T(8,128)(2,1)} %get-tuple-element.149.hn_ref, bf16[2048,1024]{1,0:T(8,128)(2,1)} %bitcast.97, bf16[1024,4096]{1,0:T(8,128)(2,1)} %bitcast.67, bf16[4096,1024]{1,0:T(8,128)(2,1)} %bitcast.77), custom_call_target="tpu_custom_call" | custom-call | flops 10737418240 | bytes 20971520 | tf_op jit(solution)/shard_map/finish/pallas_call | solution.py:279
  730.1 2.8 select_select_fusion.2
  733.2 2.4 maximum_bitcast_fusion
  735.6 3.2 copy.37
  (87 shorter events, 38.3 us)
Async XLA Ops:
  7.2 728.4 %all-reduce.2.cloned.1.call-start = ((), (), s32[]{:S(2)}) async-start(), calls=%async_computation | async-start | bytes 4194304 | tf_op jit(solution)/shard_map/psum | solution.py:296
  118.4 43.6 %collective-permute-start = (bf16[512,1024]{1,0:T(8,128)(2,1)}, bf16[512,1024]{1,0:T(8,128)(2,1)S(1)}, u32[]{:S(2)}, u32[]{:S(2)}) collective-permute-start(bf16[512,1024]{1,0:T(8,128)(2,1)} %finish.10), channel_id=1, source_target_pairs={{0,8},{8,16},{16,24},{1,9},{9,17},{17,25},{2,10},{10,18},{18,26},{... | collective-permute-start | bytes 3145736 | tf_op jit(solution)/shard_map/ppermute | solution.py:294
  158.3 26.2 %collective-permute-start.1 = (bf16[512,1024]{1,0:T(8,128)(2,1)}, bf16[512,1024]{1,0:T(8,128)(2,1)S(1)}, u32[]{:S(2)}, u32[]{:S(2)}) collective-permute-start(bf16[512,1024]{1,0:T(8,128)(2,1)} %finish.11), channel_id=1, source_target_pairs={{0,8},{8,16},{16,24},{1,9},{9,17},{17,25},{2,10},{10,18},{18,26},{... | collective-permute-start | bytes 3145736 | tf_op jit(solution)/shard_map/ppermute | solution.py:294
  263.7 41.8 %collective-permute-start.2 = (bf16[512,1024]{1,0:T(8,128)(2,1)}, bf16[512,1024]{1,0:T(8,128)(2,1)S(1)}, u32[]{:S(2)}, u32[]{:S(2)}) collective-permute-start(bf16[512,1024]{1,0:T(8,128)(2,1)} %finish.12), channel_id=1, source_target_pairs={{0,8},{8,16},{16,24},{1,9},{9,17},{17,25},{2,10},{10,18},{18,26},{... | collective-permute-start | bytes 3145736 | tf_op jit(solution)/shard_map/ppermute | solution.py:294
  303.6 26.2 %collective-permute-start.3 = (bf16[512,1024]{1,0:T(8,128)(2,1)}, bf16[512,1024]{1,0:T(8,128)(2,1)S(1)}, u32[]{:S(2)}, u32[]{:S(2)}) collective-permute-start(bf16[512,1024]{1,0:T(8,128)(2,1)} %finish.13), channel_id=1, source_target_pairs={{0,8},{8,16},{16,24},{1,9},{9,17},{17,25},{2,10},{10,18},{18,26},{... | collective-permute-start | bytes 3145736 | tf_op jit(solution)/shard_map/ppermute | solution.py:294
  305.5 1.0 copy-start.8
  329.8 1.0 copy-start.9
  407.1 40.2 %collective-permute-start.4 = (bf16[512,1024]{1,0:T(8,128)(2,1)}, bf16[512,1024]{1,0:T(8,128)(2,1)S(1)}, u32[]{:S(2)}, u32[]{:S(2)}) collective-permute-start(bf16[512,1024]{1,0:T(8,128)(2,1)} %finish.14), channel_id=1, source_target_pairs={{0,8},{8,16},{16,24},{1,9},{9,17},{17,25},{2,10},{10,18},{18,26},{... | collective-permute-start | bytes 3145736 | tf_op jit(solution)/shard_map/ppermute | solution.py:294
  445.1 26.2 %collective-permute-start.5 = (bf16[512,1024]{1,0:T(8,128)(2,1)}, bf16[512,1024]{1,0:T(8,128)(2,1)S(1)}, u32[]{:S(2)}, u32[]{:S(2)}) collective-permute-start(bf16[512,1024]{1,0:T(8,128)(2,1)} %finish.15), channel_id=1, source_target_pairs={{0,8},{8,16},{16,24},{1,9},{9,17},{17,25},{2,10},{10,18},{18,26},{... | collective-permute-start | bytes 3145736 | tf_op jit(solution)/shard_map/ppermute | solution.py:294
  447.3 1.0 copy-start.10
  471.4 1.0 copy-start.11
  548.2 40.3 %collective-permute-start.6 = (bf16[512,1024]{1,0:T(8,128)(2,1)}, bf16[512,1024]{1,0:T(8,128)(2,1)S(1)}, u32[]{:S(2)}, u32[]{:S(2)}) collective-permute-start(bf16[512,1024]{1,0:T(8,128)(2,1)} %finish.16), channel_id=1, source_target_pairs={{0,8},{8,16},{16,24},{1,9},{9,17},{17,25},{2,10},{10,18},{18,26},{... | collective-permute-start | bytes 3145736 | tf_op jit(solution)/shard_map/ppermute | solution.py:294
  586.5 26.2 %collective-permute-start.7 = (bf16[512,1024]{1,0:T(8,128)(2,1)}, bf16[512,1024]{1,0:T(8,128)(2,1)S(1)}, u32[]{:S(2)}, u32[]{:S(2)}) collective-permute-start(bf16[512,1024]{1,0:T(8,128)(2,1)} %finish.17), channel_id=1, source_target_pairs={{0,8},{8,16},{16,24},{1,9},{9,17},{17,25},{2,10},{10,18},{18,26},{... | collective-permute-start | bytes 3145736 | tf_op jit(solution)/shard_map/ppermute | solution.py:294
  588.5 1.0 copy-start.6
  612.7 1.0 copy-start.7
  613.7 40.1 %copy-start.3 = (f32[16,128,128]{2,1,0:T(8,128)S(1)}, f32[16,128,128]{2,1,0:T(8,128)}, u32[]{:S(2)}) copy-start(f32[16,128,128]{2,1,0:T(8,128)} %get-tuple-element.155) | copy-start | bytes 3145732
  613.7 40.1 %copy-start.4 = (f32[16,128,128]{2,1,0:T(8,128)S(1)}, f32[16,128,128]{2,1,0:T(8,128)}, u32[]{:S(2)}) copy-start(f32[16,128,128]{2,1,0:T(8,128)} %get-tuple-element.156) | copy-start | bytes 3145732
  613.7 40.2 %copy-start.5 = (f32[16,128,128]{2,1,0:T(8,128)S(1)}, f32[16,128,128]{2,1,0:T(8,128)}, u32[]{:S(2)}) copy-start(f32[16,128,128]{2,1,0:T(8,128)} %get-tuple-element.157) | copy-start | bytes 3145732
  709.8 20.3 %copy-start = (bf16[512,1024]{1,0:T(8,128)(2,1)S(1)}, bf16[512,1024]{1,0:T(8,128)(2,1)}, u32[]{:S(2)}) copy-start(bf16[512,1024]{1,0:T(8,128)(2,1)} %finish.10) | copy-start | bytes 3145732
  709.8 20.3 %copy-start.1 = (bf16[512,1024]{1,0:T(8,128)(2,1)S(1)}, bf16[512,1024]{1,0:T(8,128)(2,1)}, u32[]{:S(2)}) copy-start(bf16[512,1024]{1,0:T(8,128)(2,1)} %finish.11) | copy-start | bytes 3145732
  709.8 20.3 %copy-start.2 = (bf16[512,1024]{1,0:T(8,128)(2,1)S(1)}, bf16[512,1024]{1,0:T(8,128)(2,1)}, u32[]{:S(2)}) copy-start(bf16[512,1024]{1,0:T(8,128)(2,1)} %finish.12) | copy-start | bytes 3145732
Sparse Core Ops, SparseCore 0:
  657.8 58.7 all-reduce.1
